TPU v7x, 32 devices: a whole 2x2x4 slice. The times are simulated.
32 devices in a mesh: slab: 8 (over z, x), pencil: 4 (over y, core).
Axes of the slice: x: 2, y: 2, z: 4, core: 2. Of those that a mesh axis runs over, the one named last changes fastest.
Arguments:
- sample_tile: int32 [8192, 1], P(('slab', 'pencil')), may hold values from 0 to 31; in each aligned block of 256 rows (0 to 255, 256 to 511, ...) at most 16 rows name the same one
- sample_cell: int32 [3, 8192], P(None, ('slab', 'pencil')), may hold values from 0 to 511, as said below
- sample_frac: float32 [3, 8192], P(None, ('slab', 'pencil')), may hold values from 0 to 1
- sample_value: float32 [2, 8192], P(None, ('slab', 'pencil')), may hold values from -24 to 24
Outputs:
- volume: float32 [2, 64, 512, 512], P(None, None, 'slab', 'pencil')
Inputs may be any that keep to these rules, and one draw needn't show every extreme that they name: `sample_tile`: among the 256 samples of one device no tile is named more than 16 times, and that count is reached in some device's block. `sample_cell`: row 0 is below 8, row 1 below 128, row 2 below 512.
All inputs are finite; a program needn't handle non-finite values.
Results may differ from a plain program's by a relative error of at most 0.0003.
Values sent between devices are 32-bit elements; how exact they have to be, the bound alone decides.
No kernel may reach another device: no remote copies, remote signals or barrier semaphores. Data moves between devices by JAX's collectives and lax.ppermute only.
A program may use at most 64 MiB of HBM per device.

v0:
```python
import math
import jax
import jax.numpy as jnp
from jax import lax
from jax.sharding import PartitionSpec as P

NY = 512
NX = 512
PLANES = 8
beta_shape = 18.64


def from_behind(block, axis, distance):
    devices = range(lax.axis_size(axis))
    route = [((i - distance) % len(devices), i) for i in devices]
    return lax.ppermute(block, axis, route)


def bessel_zero(value):
    quarter = value * value * 0.25
    term = jnp.ones_like(value)
    total = jnp.ones_like(value)
    for order in range(1, 41):
        term = term * quarter / float(order * order)
        total = total + term
    return total


def kernel_weights(offset):
    tap_offsets = jnp.arange(8, dtype=jnp.float32) - 3.0
    scaled_gap = (tap_offsets[None, :] - offset[:, None]) * 0.25
    radicand = jnp.maximum(1.0 - scaled_gap * scaled_gap, 0.0)
    numerator = bessel_zero(beta_shape * jnp.sqrt(radicand))
    return numerator / bessel_zero(jnp.full((), beta_shape, jnp.float32))


def dft_tables(length):
    counter = jnp.arange(length, dtype=jnp.int32)
    phase_index = counter[:, None] * counter[None, :] % length
    angles = phase_index.astype(jnp.float32) * jnp.float32(2.0 * math.pi / length)
    factor = jnp.float32(1.0 / math.sqrt(length))
    cosine = jnp.cos(angles) * factor
    sine = jnp.sin(angles) * factor
    return (cosine, sine, cosine + sine)


def placed_weights(tap_weight, anchor, length, wrap):
    positions = jnp.arange(length, dtype=jnp.int32)
    placed = jnp.zeros((anchor.shape[0], length), jnp.float32)
    for tap in range(8):
        where_at = anchor + tap
        if wrap:
            where_at = where_at % length
        hit = (positions[None, :] == where_at[:, None]).astype(jnp.float32)
        placed = placed + hit * tap_weight[:, tap][:, None]
    return placed


def spread_grid(cells, records, depth_cells, row_count):
    sample_count = cells.shape[1]
    height_cells = row_count + 7
    weight_z = kernel_weights(records[0])
    weight_y = kernel_weights(records[1])
    weight_x = kernel_weights(records[2])
    plane_table = placed_weights(weight_z, cells[0], depth_cells, False)
    row_table = placed_weights(weight_y, cells[1], height_cells, False)
    column_table = placed_weights(weight_x, cells[2], NX, True)
    left_table = (plane_table[:, :, None] * row_table[:, None, :]).reshape(
        sample_count, depth_cells * height_cells
    )
    real_right = column_table * records[3][:, None]
    imag_right = column_table * records[4][:, None]
    numbers = (((0,), (0,)), ((), ()))
    real_grid = lax.dot_general(
        left_table,
        real_right,
        numbers,
        precision=lax.Precision.HIGHEST,
        preferred_element_type=jnp.float32,
    )
    imag_grid = lax.dot_general(
        left_table,
        imag_right,
        numbers,
        precision=lax.Precision.HIGHEST,
        preferred_element_type=jnp.float32,
    )
    return jnp.stack([real_grid, imag_grid]).reshape(2, depth_cells, height_cells, NX)


def product(left, right):
    return jnp.dot(left, right, precision=lax.Precision.HIGHEST, preferred_element_type=jnp.float32)


def shards(sample_tile, sample_cell, sample_frac, sample_value):
    n_slab = lax.axis_size("slab")
    n_pencil = lax.axis_size("pencil")
    tile_count = n_slab * n_pencil
    sample_count = sample_tile.shape[0]
    capacity = max(2, 2 * sample_count // tile_count)
    row_count = NY // n_pencil
    planes = PLANES
    owner_tile = sample_tile[:, 0]
    sort_order = jnp.argsort(owner_tile, stable=True)
    sorted_owner = owner_tile[sort_order]
    tile_ids = jnp.arange(tile_count, dtype=jnp.int32)
    tile_loads = jnp.sum((sorted_owner[:, None] == tile_ids[None, :]).astype(jnp.int32), axis=0)
    starts = jnp.cumsum(tile_loads) - tile_loads
    sorted_rank = jnp.arange(sample_count, dtype=jnp.int32) - starts[sorted_owner]
    slot_rank = jnp.zeros((sample_count,), jnp.int32).at[sort_order].set(sorted_rank)
    records = jnp.concatenate([sample_frac, sample_value], axis=0)
    slot_count = 2 * capacity
    next_owner = (owner_tile // n_pencil + 1) % n_slab * n_pencil + owner_tile % n_pencil
    lowered = sample_cell.at[0].add(-planes)
    first_slot = owner_tile * slot_count + slot_rank
    second_slot = next_owner * slot_count + capacity + slot_rank
    cell_buffer = jnp.zeros((3, tile_count * slot_count), jnp.int32)
    cell_buffer = cell_buffer.at[:, first_slot].set(sample_cell).at[:, second_slot].set(lowered)
    record_buffer = jnp.zeros((5, tile_count * slot_count), jnp.float32)
    record_buffer = record_buffer.at[:, first_slot].set(records).at[:, second_slot].set(records)
    cell_buffer = cell_buffer.reshape(3, n_slab, n_pencil, slot_count)
    record_buffer = record_buffer.reshape(5, n_slab, n_pencil, slot_count)
    got_cells, got_records = (
        lax.all_to_all(
            lax.all_to_all(cell_buffer, "slab", split_axis=1, concat_axis=1, tiled=True),
            "pencil",
            split_axis=2,
            concat_axis=2,
            tiled=True,
        ),
        lax.all_to_all(
            lax.all_to_all(record_buffer, "slab", split_axis=1, concat_axis=1, tiled=True),
            "pencil",
            split_axis=2,
            concat_axis=2,
            tiled=True,
        ),
    )
    field_grid = spread_grid(
        got_cells.reshape(3, -1), got_records.reshape(5, -1), planes, row_count
    )
    row_rim = from_behind(field_grid[:, :, row_count:], "pencil", 1)
    field_grid = field_grid[:, :, :row_count].at[:, :, :7].add(row_rim)
    cos_x, sin_x, both_x = dft_tables(NX)
    flat_real = field_grid[0].reshape(planes * row_count, NX)
    flat_imag = field_grid[1].reshape(planes * row_count, NX)
    first_term = product(flat_real, cos_x)
    second_term = product(flat_imag, sin_x)
    third_term = product(flat_real + flat_imag, both_x)
    turned_real = (first_term - second_term).reshape(planes, row_count, NX)
    turned_imag = (third_term - first_term - second_term).reshape(planes, row_count, NX)
    cos_y, sin_y, both_y = dft_tables(NY)
    part_real = lax.all_to_all(turned_real, "pencil", split_axis=2, concat_axis=1, tiled=True)
    part_imag = lax.all_to_all(turned_imag, "pencil", split_axis=2, concat_axis=1, tiled=True)
    first_part = jnp.einsum(
        "nyx,ym->nmx",
        part_real,
        cos_y,
        precision=lax.Precision.HIGHEST,
        preferred_element_type=jnp.float32,
    )
    second_part = jnp.einsum(
        "nyx,ym->nmx",
        part_imag,
        sin_y,
        precision=lax.Precision.HIGHEST,
        preferred_element_type=jnp.float32,
    )
    third_part = jnp.einsum(
        "nyx,ym->nmx",
        part_real + part_imag,
        both_y,
        precision=lax.Precision.HIGHEST,
        preferred_element_type=jnp.float32,
    )
    middle_real = first_part - second_part
    middle_imag = third_part - first_part - second_part
    cos_z, sin_z, both_z = dft_tables(planes * n_slab)
    part_real = lax.all_to_all(middle_real, "slab", split_axis=1, concat_axis=0, tiled=True)
    part_imag = lax.all_to_all(middle_imag, "slab", split_axis=1, concat_axis=0, tiled=True)
    first_part = jnp.einsum(
        "zyx,zm->myx",
        part_real,
        cos_z,
        precision=lax.Precision.HIGHEST,
        preferred_element_type=jnp.float32,
    )
    second_part = jnp.einsum(
        "zyx,zm->myx",
        part_imag,
        sin_z,
        precision=lax.Precision.HIGHEST,
        preferred_element_type=jnp.float32,
    )
    third_part = jnp.einsum(
        "zyx,zm->myx",
        part_real + part_imag,
        both_z,
        precision=lax.Precision.HIGHEST,
        preferred_element_type=jnp.float32,
    )
    final_real = first_part - second_part
    final_imag = third_part - first_part - second_part
    return jnp.stack([final_real, final_imag])


def solution(mesh):
    placed = (
        P(("slab", "pencil"), None),
        P(None, ("slab", "pencil")),
        P(None, ("slab", "pencil")),
        P(None, ("slab", "pencil")),
    )
    return jax.shard_map(
        shards,
        mesh=mesh,
        in_specs=placed,
        out_specs=P(None, None, "slab", "pencil"),
        check_vma=False,
    )
```

profile of v0, /device:TPU:0, one launch (start us, length us, event | category | flops | bytes accessed | tf_op | source)
XLA Modules:
  0.0 354.5 jit_solution(5115085824813003113)
XLA Ops:
  0.0 0.7 copy.108
  0.7 3.8 %sort.17 = (s32[256]{0:T(256)}, s32[256]{0:T(256)S(1)}) sort(s32[256]{0:T(256)} %bitcast.174, s32[256]{0:T(256)S(1)} %iota.109), dimensions={0}, to_apply=%region_0.0 | sort | flops 2048 | bytes 4096 | tf_op jit(solution)/shard_map/jit(argsort)/sort | solution.py:104
  4.6 2.0 gather_fusion
  7.0 0.7 fusion.151
  7.7 0.7 fusion.150
  8.4 4.3 %compare_select_fusion.1 = (s32[256,1]{0,1:T(1,128)S(1)}, s32[256,1]{0,1:T(1,128)S(1)}) fusion(s32[]{:T(128)} %bitcast.30, s32[]{:T(128)} %bitcast.31, s32[]{:T(128)} %bitcast.32, s32[]{:T(128)} %bitcast.33, s32[]{:T(128)} %bitcast.34, s32[]{:T(128)} %bitcast.36, s32[]{:T(128)} %bitcast.35, s32[256,1]{0,1:T(1,128)S(1)} %bitcast.236), kind=kLoop, calls=%fused_computation.186 | loop fusion | flops 3840 | bytes 3100 | tf_op jit(solution)/shard_map/gather | solution.py:109
  12.9 15.7 %select_subtract_fusion = s32[256]{0:T(256)S(1)} fusion(pred[256]{0:T(512)(128)(4,1)S(1)} %get-tuple-element.55, pred[256]{0:T(512)(128)(4,1)S(1)} %get-tuple-element.54, pred[256]{0:T(512)(128)(4,1)S(1)} %get-tuple-element.53, pred[256]{0:T(512)(128)(4,1)S(1)} %get-tuple-element.52, pred[256]{0:T(512)(128)(4,1)S(1)} %get-tuple-element.51, ...), kind=kLoop, calls=%fused_computation.220 | loop fusion | flops 6656 | bytes 8548 | tf_op jit(solution)/shard_map/sub | solution.py:109
  28.6 1.4 scatter_custom_fusion
  30.0 0.7 compare_select_fusion.7
  31.0 1.3 scatter_custom_fusion.1
  32.3 1.4 scatter_fusion
  34.0 0.7 reshape.1138
  34.7 7.3 %all-to-all-start = ((s32[8,1,384]{2,1,0:T(1,128)}), s32[8,1,384]{2,1,0:T(1,128)S(1)}, u32[]{:S(2)}, u32[]{:S(2)}) async-start(s32[8,1,384]{2,1,0:T(1,128)} %reshape.1138), calls=%async_computation | async-start | bytes 24576 | tf_op jit(solution)/shard_map/all_to_all | solution.py:125
  42.0 6.5 %all-to-all-done = s32[8,1,384]{2,1,0:T(1,128)S(1)} async-done(((s32[8,1,384]{2,1,0:T(1,128)}), s32[8,1,384]{2,1,0:T(1,128)S(1)}, u32[]{:S(2)}, u32[]{:S(2)}) %all-to-all-start) | async-done | bytes 12320 | tf_op jit(solution)/shard_map/all_to_all | solution.py:125
  49.0 0.6 reduce.57
  49.7 0.7 reshape.1140
  50.4 3.2 all-to-all-start.1
  53.8 1.3 scatter_custom_fusion.3
  55.1 1.4 scatter_fusion.1
  56.7 0.7 reshape.1134
  57.5 3.3 all-to-all-start.2
  60.8 0.6 reduce.58
  61.8 5.5 %all-to-all-done.2 = f32[8,1,640]{2,1,0:T(1,128)S(1)} async-done(((f32[8,1,640]{2,1,0:T(1,128)}), f32[8,1,640]{2,1,0:T(1,128)S(1)}, u32[]{:S(2)}, u32[]{:S(2)}) %all-to-all-start.2) | async-done | bytes 20512 | tf_op jit(solution)/shard_map/all_to_all | solution.py:132
  67.4 0.6 broadcast.1677
  68.0 0.7 reduce.55
  68.8 0.7 reshape.1136
  69.5 3.5 %all-to-all-start.3 = ((f32[4,1,1280]{2,1,0:T(1,128)}), f32[4,1,1280]{2,1,0:T(1,128)S(1)}, u32[]{:S(2)}, u32[]{:S(2)}) async-start(f32[4,1,1280]{2,1,0:T(1,128)} %reshape.1136), calls=%async_computation.3 | async-start | bytes 40960 | tf_op jit(solution)/shard_map/all_to_all | solution.py:131
  73.1 3.6 %all-to-all-done.3 = f32[4,1,1280]{2,1,0:T(1,128)S(1)} async-done(((f32[4,1,1280]{2,1,0:T(1,128)}), f32[4,1,1280]{2,1,0:T(1,128)S(1)}, u32[]{:S(2)}, u32[]{:S(2)}) %all-to-all-start.3) | async-done | bytes 20512 | tf_op jit(solution)/shard_map/all_to_all | solution.py:131
  76.7 0.7 reduce.56
  79.1 2.6 broadcast_multiply_fusion
  81.7 4.9 %mul.941 = f32[1024,1080]{0,1:T(8,128)} reshape(f32[1024,8,135]{0,2,1:T(8,128)} %broadcast_multiply_fusion) | data formatting | bytes 8847360 | tf_op jit(solution)/shard_map/mul | solution.py:68
  86.6 4.8 %reshape.921 = f32[8,135,1024]{2,1,0:T(8,128)} reshape(f32[1080,1024]{1,0:T(8,128)} %bitcast.183) | data formatting | bytes 8847360 | tf_op jit(solution)/shard_map/reshape.869
  91.4 11.9 %fusion.25 = f32[1,8,135,512]{3,2,1,0:T(8,128)S(1)} fusion(f32[8,135,1024]{2,1,0:T(8,128)} %reshape.921, f32[1024]{0:T(1024)S(1)} %mul.1013, f32[1024]{0:T(1024)S(1)} %bitcast.222, s32[1024]{0:T(1024)S(1)} %get-tuple-element.99, f32[1024]{0:T(1024)S(1)} %bitcast.224, s32[1024]{0:T(1024)S(1)} %get-tuple-element.98, f32[1024]{0:T(1024)S(1)} %bitcast.226, ...), kind=kOutput, calls=%fused_computation.50 | convolution fusion | flops 6807355392 | bytes 6705152 | tf_op jit(solution)/shard_map/dot_general | solution.py:81
  103.3 10.0 %fusion.22 = f32[1,8,135,512]{3,2,1,0:T(8,128)S(1)} fusion(f32[8,135,1024]{2,1,0:T(8,128)S(1)} %copy-done.5, f32[1024]{0:T(1024)S(1)} %mul.1010, f32[1024]{0:T(1024)S(1)} %bitcast.223, s32[1024]{0:T(1024)S(1)} %get-tuple-element.99, f32[1024]{0:T(1024)S(1)} %bitcast.225, s32[1024]{0:T(1024)S(1)} %get-tuple-element.98, f32[1024]{0:T(1024)S(1)} %bitcast.227, ...), kind=kOutput, calls=%fused_computation.49 | convolution fusion | flops 6807355392 | bytes 6705152 | tf_op jit(solution)/shard_map/dot_general | solution.py:74
  113.4 2.5 fusion
  115.9 3.3 collective-permute-done
  119.2 2.0 scatter-add.9
  121.2 2.9 fusion.144
  124.1 8.4 %fusion.47 = f32[1024,512]{1,0:T(8,128)S(1)} fusion(f32[1024,512]{1,0:T(8,128)S(1)} %bitcast.188), kind=kOutput, calls=%fused_computation.71 | convolution fusion | flops 3225157632 | bytes 4194304 | tf_op jit(solution)/shard_map/dot_general | solution.py:92
  132.6 8.6 %fusion.152 = (f32[1024,512]{1,0:T(8,128)}, f32[1024,512]{1,0:T(8,128)S(1)}) fusion(f32[1024,512]{1,0:T(8,128)S(1)} %fusion.47, f32[1024,512]{1,0:T(8,128)S(1)} %bitcast.181), kind=kOutput, calls=%fused_computation.280 | convolution fusion | flops 3225681920 | bytes 8388608 | tf_op jit(solution)/shard_map/dot_general | solution.py:92
  141.2 7.9 %subtract_subtract_fusion = f32[1024,512]{1,0:T(8,128)S(1)} fusion(f32[1024,512]{1,0:T(8,128)S(1)} %fusion.47, f32[1024,512]{1,0:T(8,128)S(1)} %get-tuple-element.152, f32[1024,512]{1,0:T(8,128)S(1)} %bitcast.182, f32[1024,512]{1,0:T(8,128)S(1)} %bitcast.189), kind=kOutput, calls=%fused_computation.31 | convolution fusion | flops 3227254784 | bytes 10485760 | tf_op jit(solution)/shard_map/dot_general | solution.py:92
  149.1 1.9 copy.72
  151.0 3.6 %all-to-all-start.5 = ((f32[8,128,512]{1,0,2:T(8,128)}), f32[8,128,512]{1,0,2:T(8,128)S(1)}, u32[]{:S(2)}, u32[]{:S(2)}) async-start(f32[8,128,512]{1,0,2:T(8,128)} %copy.72), calls=%async_computation.5 | async-start | bytes 4194304 | tf_op jit(solution)/shard_map/all_to_all | solution.py:154
  154.6 2.9 copy.70
  157.5 22.7 %all-to-all-done.5 = f32[8,128,512]{1,0,2:T(8,128)S(1)} async-done(((f32[8,128,512]{1,0,2:T(8,128)}), f32[8,128,512]{1,0,2:T(8,128)S(1)}, u32[]{:S(2)}, u32[]{:S(2)}) %all-to-all-start.5) | async-done | bytes 2097184 | tf_op jit(solution)/shard_map/all_to_all | solution.py:154
  180.2 1.3 copy-done.3
  181.6 4.8 %all-to-all-start.4 = ((f32[8,128,512]{1,0,2:T(8,128)}), f32[8,128,512]{1,0,2:T(8,128)}, u32[]{:S(2)}, u32[]{:S(2)}) async-start(f32[8,128,512]{1,0,2:T(8,128)} %copy.70), calls=%async_computation.4 | async-start | bytes 4194304 | tf_op jit(solution)/shard_map/all_to_all | solution.py:153
  186.4 1.9 copy.73
  188.4 23.8 %all-to-all-done.4 = f32[8,128,512]{1,0,2:T(8,128)} async-done(((f32[8,128,512]{1,0,2:T(8,128)}), f32[8,128,512]{1,0,2:T(8,128)}, u32[]{:S(2)}, u32[]{:S(2)}) %all-to-all-start.4) | async-done | bytes 2097184 | tf_op jit(solution)/shard_map/all_to_all | solution.py:153
  212.1 2.9 copy.71
  215.0 9.0 %fusion.38 = f32[512,8,128]{2,0,1:T(8,128)S(1)} fusion(f32[8,512,128]{2,1,0:T(8,128)} %bitcast.184), kind=kOutput, calls=%fused_computation.60 | convolution fusion | flops 3225157632 | bytes 4194304 | tf_op jit(solution)/shard_map/nyx,ym->nmx/dot_general | solution.py:155
  224.0 9.2 %bitcast_subtract_fusion.1 = (f32[8,512,128]{2,1,0:T(8,128)S(1)}, f32[512,8,128]{2,0,1:T(8,128)}) fusion(f32[512,8,128]{2,0,1:T(8,128)S(1)} %fusion.38, f32[8,512,128]{2,1,0:T(8,128)S(1)} %bitcast.179), kind=kOutput, calls=%fused_computation.22 | convolution fusion | flops 3225681920 | bytes 8388608 | tf_op jit(solution)/shard_map/nyx,ym->nmx/dot_general | solution.py:162
  233.2 2.6 copy.74
  235.7 3.6 %all-to-all-start.6 = ((f32[8,512,128]{2,0,1:T(8,128)}), f32[8,512,128]{2,0,1:T(8,128)S(1)}, u32[]{:S(2)}, u32[]{:S(2)}) async-start(f32[8,512,128]{2,0,1:T(8,128)} %copy.74), calls=%async_computation.6 | async-start | bytes 4194304 | tf_op jit(solution)/shard_map/all_to_all | solution.py:179
  239.3 11.1 %fusion.7 = f32[8,512,128]{2,1,0:T(8,128)S(1)} fusion(f32[512,8,128]{2,0,1:T(8,128)} %get-tuple-element.154, f32[512,8,128]{2,0,1:T(8,128)} %copy-done.4, f32[8,512,128]{2,1,0:T(8,128)} %bitcast.185, f32[8,512,128]{2,1,0:T(8,128)} %bitcast.180), kind=kOutput, calls=%fused_computation.21 | convolution fusion | flops 3227254784 | bytes 10485760 | tf_op jit(solution)/shard_map/nyx,ym->nmx/dot_general | solution.py:169
  250.5 2.5 copy.76
  253.0 34.5 %all-to-all-done.6 = f32[8,512,128]{2,0,1:T(8,128)S(1)} async-done(((f32[8,512,128]{2,0,1:T(8,128)}), f32[8,512,128]{2,0,1:T(8,128)S(1)}, u32[]{:S(2)}, u32[]{:S(2)}) %all-to-all-start.6) | async-done | bytes 2097184 | tf_op jit(solution)/shard_map/all_to_all | solution.py:179
  287.5 1.3 copy-done
  288.8 4.6 %all-to-all-start.7 = ((f32[8,512,128]{2,0,1:T(8,128)}), f32[8,512,128]{2,0,1:T(8,128)}, u32[]{:S(2)}, u32[]{:S(2)}) async-start(f32[8,512,128]{2,0,1:T(8,128)} %copy.76), calls=%async_computation.7 | async-start | bytes 4194304 | tf_op jit(solution)/shard_map/all_to_all | solution.py:180
  293.3 3.6 %fusion.5 = f32[64,64,128]{2,0,1:T(8,128)S(1)} fusion(f32[8,8,64,128]{3,0,2,1:T(8,128)} %bitcast.177), kind=kOutput, calls=%fused_computation.18 | convolution fusion | flops 402714624 | bytes 4194304 | tf_op jit(solution)/shard_map/zyx,zm->myx/dot_general | solution.py:181
  296.9 44.2 %all-to-all-done.7 = f32[8,512,128]{2,0,1:T(8,128)} async-done(((f32[8,512,128]{2,0,1:T(8,128)}), f32[8,512,128]{2,0,1:T(8,128)}, u32[]{:S(2)}, u32[]{:S(2)}) %all-to-all-start.7) | async-done | bytes 2097184 | tf_op jit(solution)/shard_map/all_to_all | solution.py:180
  341.1 3.7 %fusion.1 = f32[64,64,128]{2,0,1:T(8,128)S(1)} fusion(f32[8,8,64,128]{3,0,2,1:T(8,128)} %bitcast.93), kind=kOutput, calls=%fused_computation.14 | convolution fusion | flops 402714624 | bytes 4194304 | tf_op jit(solution)/shard_map/zyx,zm->myx/dot_general | solution.py:188
  344.9 3.9 %subtract_bitcast_fusion = f32[1,64,64,128]{3,1,2,0:T(8,128)S(1)} fusion(f32[64,64,128]{2,0,1:T(8,128)S(1)} %fusion.1, f32[64,64,128]{2,0,1:T(8,128)S(1)} %fusion.5, f32[8,8,64,128]{3,0,2,1:T(8,128)} %bitcast.93, f32[8,8,64,128]{3,0,2,1:T(8,128)S(1)} %bitcast.178), kind=kOutput, calls=%fused_computation.27 | convolution fusion | flops 404295680 | bytes 10485760 | tf_op jit(solution)/shard_map/zyx,zm->myx/dot_general | solution.py:195
  349.8 4.4 %copy.78 = f32[2,64,64,128]{3,2,1,0:T(8,128)} copy(f32[2,64,64,128]{3,1,2,0:T(8,128)S(1)} %pad_maximum_fusion) | data formatting | bytes 8388608 | tf_op jit(solution)/shard_map/stack | solution.py:204
  (71 shorter events, 5.3 us)
Async XLA Ops:
  0.0 42.0 %copy-start.6 = (f32[3,256]{1,0:T(4,128)S(1)}, f32[3,256]{1,0:T(4,128)}, u32[]{:S(2)}) copy-start(f32[3,256]{1,0:T(4,128)} %param.10) | copy-start | bytes 9220
  0.0 42.0 %copy-start.7 = (f32[2,256]{1,0:T(2,128)S(1)}, f32[2,256]{1,0:T(2,128)}, u32[]{:S(2)}) copy-start(f32[2,256]{1,0:T(2,128)} %param.11) | copy-start | bytes 6148
  34.7 13.8 %all-to-all-start = ((s32[8,1,384]{2,1,0:T(1,128)}), s32[8,1,384]{2,1,0:T(1,128)S(1)}, u32[]{:S(2)}, u32[]{:S(2)}) async-start(s32[8,1,384]{2,1,0:T(1,128)} %reshape.1138), calls=%async_computation | async-start | bytes 24576 | tf_op jit(solution)/shard_map/all_to_all | solution.py:125
  50.4 7.1 %all-to-all-start.1 = ((s32[4,1,768]{2,1,0:T(1,128)}), s32[4,1,768]{2,1,0:T(1,128)S(1)}, u32[]{:S(2)}, u32[]{:S(2)}) async-start(s32[4,1,768]{2,1,0:T(1,128)} %reshape.1140), calls=%async_computation.1 | async-start | bytes 24576 | tf_op jit(solution)/shard_map/all_to_all | solution.py:124
  57.5 9.9 %all-to-all-start.2 = ((f32[8,1,640]{2,1,0:T(1,128)}), f32[8,1,640]{2,1,0:T(1,128)S(1)}, u32[]{:S(2)}, u32[]{:S(2)}) async-start(f32[8,1,640]{2,1,0:T(1,128)} %reshape.1134), calls=%async_computation.2 | async-start | bytes 40960 | tf_op jit(solution)/shard_map/all_to_all | solution.py:132
  69.5 7.1 %all-to-all-start.3 = ((f32[4,1,1280]{2,1,0:T(1,128)}), f32[4,1,1280]{2,1,0:T(1,128)S(1)}, u32[]{:S(2)}, u32[]{:S(2)}) async-start(f32[4,1,1280]{2,1,0:T(1,128)} %reshape.1136), calls=%async_computation.3 | async-start | bytes 40960 | tf_op jit(solution)/shard_map/all_to_all | solution.py:131
  91.4 11.9 %copy-start.5 = (f32[8,135,1024]{2,1,0:T(8,128)S(1)}, f32[8,135,1024]{2,1,0:T(8,128)}, u32[]{:S(2)}) copy-start(f32[8,135,1024]{2,1,0:T(8,128)} %reshape.921) | copy-start | bytes 13271044
  113.3 5.8 %collective-permute-start = (f32[2,8,7,512]{3,2,1,0:T(8,128)S(1)}, f32[2,8,7,512]{3,2,1,0:T(8,128)S(1)}, u32[]{:S(2)}, u32[]{:S(2)}) collective-permute-start(f32[2,8,7,512]{3,2,1,0:T(8,128)S(1)} %pad_maximum_fusion.1), channel_id=1, source_target_pairs={{3,0},{0,1},{1,2},{2,3},{7,4},{4,5},{5,6},{6,7},{11,8},{8,9},{9,10... | collective-permute-start | bytes 688136 | tf_op jit(solution)/shard_map/ppermute | solution.py:16
  151.0 29.2 %all-to-all-start.5 = ((f32[8,128,512]{1,0,2:T(8,128)}), f32[8,128,512]{1,0,2:T(8,128)S(1)}, u32[]{:S(2)}, u32[]{:S(2)}) async-start(f32[8,128,512]{1,0,2:T(8,128)} %copy.72), calls=%async_computation.5 | async-start | bytes 4194304 | tf_op jit(solution)/shard_map/all_to_all | solution.py:154
  180.2 1.3 copy-start.3
  181.6 30.6 %all-to-all-start.4 = ((f32[8,128,512]{1,0,2:T(8,128)}), f32[8,128,512]{1,0,2:T(8,128)}, u32[]{:S(2)}, u32[]{:S(2)}) async-start(f32[8,128,512]{1,0,2:T(8,128)} %copy.70), calls=%async_computation.4 | async-start | bytes 4194304 | tf_op jit(solution)/shard_map/all_to_all | solution.py:153
  188.4 35.6 %copy-start.2 = (f32[8,128,4,128]{3,1,2,0:T(8,128)}, f32[8,128,4,128]{3,1,2,0:T(8,128)S(1)}, u32[]{:S(2)}) copy-start(f32[8,128,4,128]{3,1,2,0:T(8,128)S(1)} %copy.73) | copy-start | bytes 6291460
  224.0 9.2 %copy-start.4 = (f32[512,8,128]{2,0,1:T(8,128)}, f32[512,8,128]{2,0,1:T(8,128)S(1)}, u32[]{:S(2)}) copy-start(f32[512,8,128]{2,0,1:T(8,128)S(1)} %fusion.38) | copy-start | bytes 6291460
  235.7 51.7 %all-to-all-start.6 = ((f32[8,512,128]{2,0,1:T(8,128)}), f32[8,512,128]{2,0,1:T(8,128)S(1)}, u32[]{:S(2)}, u32[]{:S(2)}) async-start(f32[8,512,128]{2,0,1:T(8,128)} %copy.74), calls=%async_computation.6 | async-start | bytes 4194304 | tf_op jit(solution)/shard_map/all_to_all | solution.py:179
  287.5 1.3 copy-start
  288.8 52.4 %all-to-all-start.7 = ((f32[8,512,128]{2,0,1:T(8,128)}), f32[8,512,128]{2,0,1:T(8,128)}, u32[]{:S(2)}, u32[]{:S(2)}) async-start(f32[8,512,128]{2,0,1:T(8,128)} %copy.76), calls=%async_computation.7 | async-start | bytes 4194304 | tf_op jit(solution)/shard_map/all_to_all | solution.py:180
  341.1 3.8 %copy-start.1 = (f32[8,512,128]{2,0,1:T(8,128)S(1)}, f32[8,512,128]{2,0,1:T(8,128)}, u32[]{:S(2)}) copy-start(f32[8,512,128]{2,0,1:T(8,128)} %copy-done) | copy-start | bytes 6291460
where the time goes:
time: 361 us; the launch traced here: 354 us
  waiting for transfers between devices  144 us (40%)
  matrix products  87.3 us (24%)
  local copies, waits for them, and re-layouts  53.4 us (15%)
  other arithmetic  34.9 us (10%)
  starting transfers between devices  34.1 us (9%)
    all_to_all x1, waiting for transfers between devices, shards(): lax.all_to_all(middle_imag, 'slab', split_axis=1, concat_axis=0, tiled=True)  44.2 us
    all_to_all x1, waiting for transfers between devices, shards(): lax.all_to_all(middle_real, 'slab', split_axis=1, concat_axis=0, tiled=True)  34.5 us
    dot_general x3, matrix products, product(): jnp.dot(left, right, precision=lax.Precision.HIGHEST, preferred_element_t...  25 us
    all_to_all x1, waiting for transfers between devices, shards(): lax.all_to_all(turned_real, 'pencil', split_axis=2, concat_axis=1, tiled=...  23.8 us
    all_to_all x1, waiting for transfers between devices, shards(): lax.all_to_all(turned_imag, 'pencil', split_axis=2, concat_axis=1, tiled=...  22.7 us
    sub x1, other arithmetic, shards(): jnp.arange(sample_count, dtype=jnp.int32) - starts[sorted_owner]  15.7 us
    dot_general x1, matrix products, spread_grid(): lax.dot_general(left_table, imag_right, numbers, precision=lax.Precision....  11.9 us
    dot_general x1, matrix products, shards(): jnp.einsum('nyx,ym->nmx', part_real + part_imag, both_y, precision=lax.Pr...  11.1 us
  transfers between devices with their start and end apart: 9, of which 8 were waited for; matrix products, arithmetic and copies ran while one was open for 8% of the time, Pallas kernels for 0%

commit v1 on v0

--- a/solution.py
+++ b/solution.py
@@ -8,6 +8,22 @@
 NX = 512
 PLANES = 8
 beta_shape = 18.64
+
+
+def exchange_in_pairs(x, axis, split, join):
+    ways, here = (lax.axis_size(axis), lax.axis_index(axis))
+    width = x.shape[split] // ways
+    shape = list(x.shape)
+    shape[split] = width
+    height = shape[join]
+    shape[join] = height * ways
+    full = jnp.zeros(shape, x.dtype)
+    for mask in range(ways):
+        part = lax.dynamic_slice_in_dim(x, (here ^ mask) * width, width, axis=split)
+        if mask:
+            part = lax.ppermute(part, axis, [(d, d ^ mask) for d in range(ways)])
+        full = lax.dynamic_update_slice_in_dim(full, part, (here ^ mask) * height, axis=join)
+    return full
 
 
 def from_behind(block, axis, distance):
@@ -121,12 +137,11 @@
     cell_buffer = cell_buffer.reshape(3, n_slab, n_pencil, slot_count)
     record_buffer = record_buffer.reshape(5, n_slab, n_pencil, slot_count)
     got_cells, got_records = (
-        lax.all_to_all(
+        exchange_in_pairs(
             lax.all_to_all(cell_buffer, "slab", split_axis=1, concat_axis=1, tiled=True),
             "pencil",
-            split_axis=2,
-            concat_axis=2,
-            tiled=True,
+            2,
+            2,
         ),
         lax.all_to_all(
             lax.all_to_all(record_buffer, "slab", split_axis=1, concat_axis=1, tiled=True),

time: 361 us -> 353 us (0.978)
  waiting for transfers between devices: 144 us -> 137 us
    all_to_all x1, waiting for transfers between devices: 5.52 us -> 0.75 us  [shards(): lax.all_to_all(record_buffer, 'slab', split_axis=1, concat_axis=1, tiled=...]
    all_to_all x1, waiting for transfers between devices: 6.52 us -> 2.69 us  [shards(): lax.all_to_all(cell_buffer, 'slab', split_axis=1, concat_axis=1, tiled=True)]
  transfers between devices with their start and end apart: 9 -> 11, of which waited for: 8 -> 10; matrix products, arithmetic and copies ran while one was open for 8% -> 9% of each run, Pallas kernels for 0% -> 0%
where the time goes in v1:
time: 353 us; the launch traced here: 347 us
  waiting for transfers between devices  137 us (39%)
  matrix products  87.2 us (25%)
  local copies, waits for them, and re-layouts  53.1 us (15%)
  other arithmetic  34.4 us (10%)
  starting transfers between devices  34.3 us (10%)
    all_to_all x1, waiting for transfers between devices, shards(): lax.all_to_all(middle_imag, 'slab', split_axis=1, concat_axis=0, tiled=True)  44.2 us
    all_to_all x1, waiting for transfers between devices, shards(): lax.all_to_all(middle_real, 'slab', split_axis=1, concat_axis=0, tiled=True)  34.3 us
    dot_general x3, matrix products, product(): jnp.dot(left, right, precision=lax.Precision.HIGHEST, preferred_element_t...  25.1 us
    all_to_all x1, waiting for transfers between devices, shards(): lax.all_to_all(turned_real, 'pencil', split_axis=2, concat_axis=1, tiled=...  23.8 us
    all_to_all x1, waiting for transfers between devices, shards(): lax.all_to_all(turned_imag, 'pencil', split_axis=2, concat_axis=1, tiled=...  22.7 us
    sub x1, other arithmetic, shards(): jnp.arange(sample_count, dtype=jnp.int32) - starts[sorted_owner]  15.7 us
    dot_general x1, matrix products, spread_grid(): lax.dot_general(left_table, imag_right, numbers, precision=lax.Precision....  11.9 us
    dot_general x1, matrix products, shards(): jnp.einsum('nyx,ym->nmx', part_real + part_imag, both_y, precision=lax.Pr...  11.1 us
  transfers between devices with their start and end apart: 11, of which 10 were waited for; matrix products, arithmetic and copies ran while one was open for 9% of the time, Pallas kernels for 0%

profile of v1, /device:TPU:0, one launch (start us, length us, event | category | flops | bytes accessed | tf_op | source)
XLA Modules:
  0.0 346.7 jit_solution(2383753456744359640)
XLA Ops:
  0.0 0.7 copy.110
  0.7 3.8 %sort.17 = (s32[256]{0:T(256)}, s32[256]{0:T(256)S(1)}) sort(s32[256]{0:T(256)} %bitcast.170, s32[256]{0:T(256)S(1)} %iota.109), dimensions={0}, to_apply=%region_0.0 | sort | flops 2048 | bytes 4096 | tf_op jit(solution)/shard_map/jit(argsort)/sort | solution.py:120
  4.6 2.0 gather_fusion
  7.0 0.7 fusion.151
  7.7 0.7 fusion.150
  8.4 4.3 %compare_select_fusion.1 = (s32[256,1]{0,1:T(1,128)S(1)}, s32[256,1]{0,1:T(1,128)S(1)}) fusion(s32[]{:T(128)} %bitcast.30, s32[]{:T(128)} %bitcast.31, s32[]{:T(128)} %bitcast.32, s32[]{:T(128)} %bitcast.33, s32[]{:T(128)} %bitcast.34, s32[]{:T(128)} %bitcast.36, s32[]{:T(128)} %bitcast.35, s32[256,1]{0,1:T(1,128)S(1)} %bitcast.230), kind=kLoop, calls=%fused_computation.186 | loop fusion | flops 3840 | bytes 3100 | tf_op jit(solution)/shard_map/gather | solution.py:125
  12.9 15.7 %select_subtract_fusion = s32[256]{0:T(256)S(1)} fusion(pred[256]{0:T(512)(128)(4,1)S(1)} %get-tuple-element.55, pred[256]{0:T(512)(128)(4,1)S(1)} %get-tuple-element.54, pred[256]{0:T(512)(128)(4,1)S(1)} %get-tuple-element.53, pred[256]{0:T(512)(128)(4,1)S(1)} %get-tuple-element.52, pred[256]{0:T(512)(128)(4,1)S(1)} %get-tuple-element.51, ...), kind=kLoop, calls=%fused_computation.220 | loop fusion | flops 6656 | bytes 8548 | tf_op jit(solution)/shard_map/sub | solution.py:125
  28.6 1.4 scatter_custom_fusion
  30.0 0.7 compare_select_fusion.7
  31.0 1.3 scatter_custom_fusion.1
  32.3 1.4 scatter_fusion
  34.0 0.7 reshape.1138
  34.7 7.3 %all-to-all-start = ((s32[8,1,384]{2,1,0:T(1,128)}), s32[8,1,384]{2,1,0:T(1,128)S(1)}, u32[]{:S(2)}, u32[]{:S(2)}) async-start(s32[8,1,384]{2,1,0:T(1,128)} %reshape.1138), calls=%async_computation | async-start | bytes 24576 | tf_op jit(solution)/shard_map/all_to_all | solution.py:141
  42.1 1.3 scatter_custom_fusion.3
  43.4 1.4 scatter_fusion.1
  45.1 0.7 reshape.1134
  45.8 2.7 all-to-all-done
  48.5 3.3 all-to-all-start.1
  51.8 0.6 broadcast.1679
  52.4 0.7 reduce.57
  53.5 1.5 collective-permute-start.1
  55.4 0.8 collective-permute-done
  56.3 0.9 collective-permute-done.1
  57.7 0.8 all-to-all-done.1
  59.0 0.7 reduce.55
  59.9 0.7 reshape.1136
  60.6 3.7 %all-to-all-start.2 = ((f32[4,1,1280]{2,1,0:T(1,128)}), f32[4,1,1280]{2,1,0:T(1,128)S(1)}, u32[]{:S(2)}, u32[]{:S(2)}) async-start(f32[4,1,1280]{2,1,0:T(1,128)} %reshape.1136), calls=%async_computation.2 | async-start | bytes 40960 | tf_op jit(solution)/shard_map/all_to_all | solution.py:146
  64.3 3.4 all-to-all-done.2
  67.7 0.7 reduce.56
  70.1 2.6 broadcast_multiply_fusion
  72.7 4.9 %mul.941 = f32[1024,1080]{0,1:T(8,128)} reshape(f32[1024,8,135]{0,2,1:T(8,128)} %broadcast_multiply_fusion) | data formatting | bytes 8847360 | tf_op jit(solution)/shard_map/mul | solution.py:84
  77.6 4.8 %reshape.921 = f32[8,135,1024]{2,1,0:T(8,128)} reshape(f32[1080,1024]{1,0:T(8,128)} %bitcast.179) | data formatting | bytes 8847360 | tf_op jit(solution)/shard_map/reshape.869
  82.4 11.9 %fusion.25 = f32[1,8,135,512]{3,2,1,0:T(8,128)S(1)} fusion(f32[8,135,1024]{2,1,0:T(8,128)} %reshape.921, f32[1024]{0:T(1024)S(1)} %mul.1013, f32[1024]{0:T(1024)S(1)} %bitcast.216, s32[1024]{0:T(1024)S(1)} %get-tuple-element.103, f32[1024]{0:T(1024)S(1)} %bitcast.218, s32[1024]{0:T(1024)S(1)} %get-tuple-element.102, f32[1024]{0:T(1024)S(1)} %bitcast.220, ...), kind=kOutput, calls=%fused_computation.50 | convolution fusion | flops 6807355392 | bytes 6705152 | tf_op jit(solution)/shard_map/dot_general | solution.py:97
  94.3 9.7 %fusion.22 = f32[1,8,135,512]{3,2,1,0:T(8,128)S(1)} fusion(f32[8,135,1024]{2,1,0:T(8,128)S(1)} %copy-done.5, f32[1024]{0:T(1024)S(1)} %mul.1010, f32[1024]{0:T(1024)S(1)} %bitcast.217, s32[1024]{0:T(1024)S(1)} %get-tuple-element.103, f32[1024]{0:T(1024)S(1)} %bitcast.219, s32[1024]{0:T(1024)S(1)} %get-tuple-element.102, f32[1024]{0:T(1024)S(1)} %bitcast.221, ...), kind=kOutput, calls=%fused_computation.49 | convolution fusion | flops 6807355392 | bytes 6705152 | tf_op jit(solution)/shard_map/dot_general | solution.py:90
  104.1 2.5 fusion
  106.6 3.3 collective-permute-done.3
  109.9 2.0 scatter-add.9
  111.9 2.9 fusion.144
  114.8 8.4 %fusion.47 = f32[1024,512]{1,0:T(8,128)S(1)} fusion(f32[1024,512]{1,0:T(8,128)S(1)} %bitcast.184), kind=kOutput, calls=%fused_computation.71 | convolution fusion | flops 3225157632 | bytes 4194304 | tf_op jit(solution)/shard_map/dot_general | solution.py:108
  123.3 8.8 %fusion.152 = (f32[1024,512]{1,0:T(8,128)}, f32[1024,512]{1,0:T(8,128)S(1)}) fusion(f32[1024,512]{1,0:T(8,128)S(1)} %fusion.47, f32[1024,512]{1,0:T(8,128)S(1)} %bitcast.177), kind=kOutput, calls=%fused_computation.284 | convolution fusion | flops 3225681920 | bytes 8388608 | tf_op jit(solution)/shard_map/dot_general | solution.py:108
  132.1 7.9 %subtract_subtract_fusion = f32[1024,512]{1,0:T(8,128)S(1)} fusion(f32[1024,512]{1,0:T(8,128)S(1)} %fusion.47, f32[1024,512]{1,0:T(8,128)S(1)} %get-tuple-element.156, f32[1024,512]{1,0:T(8,128)S(1)} %bitcast.178, f32[1024,512]{1,0:T(8,128)S(1)} %bitcast.185), kind=kOutput, calls=%fused_computation.31 | convolution fusion | flops 3227254784 | bytes 10485760 | tf_op jit(solution)/shard_map/dot_general | solution.py:108
  140.0 1.9 copy.72
  141.9 3.6 %all-to-all-start.4 = ((f32[8,128,512]{1,0,2:T(8,128)}), f32[8,128,512]{1,0,2:T(8,128)S(1)}, u32[]{:S(2)}, u32[]{:S(2)}) async-start(f32[8,128,512]{1,0,2:T(8,128)} %copy.72), calls=%async_computation.4 | async-start | bytes 4194304 | tf_op jit(solution)/shard_map/all_to_all | solution.py:169
  145.5 2.9 copy.70
  148.4 22.7 %all-to-all-done.4 = f32[8,128,512]{1,0,2:T(8,128)S(1)} async-done(((f32[8,128,512]{1,0,2:T(8,128)}), f32[8,128,512]{1,0,2:T(8,128)S(1)}, u32[]{:S(2)}, u32[]{:S(2)}) %all-to-all-start.4) | async-done | bytes 2097184 | tf_op jit(solution)/shard_map/all_to_all | solution.py:169
  171.1 1.3 copy-done.3
  172.5 4.6 %all-to-all-start.3 = ((f32[8,128,512]{1,0,2:T(8,128)}), f32[8,128,512]{1,0,2:T(8,128)}, u32[]{:S(2)}, u32[]{:S(2)}) async-start(f32[8,128,512]{1,0,2:T(8,128)} %copy.70), calls=%async_computation.3 | async-start | bytes 4194304 | tf_op jit(solution)/shard_map/all_to_all | solution.py:168
  177.1 1.9 copy.73
  179.0 23.8 %all-to-all-done.3 = f32[8,128,512]{1,0,2:T(8,128)} async-done(((f32[8,128,512]{1,0,2:T(8,128)}), f32[8,128,512]{1,0,2:T(8,128)}, u32[]{:S(2)}, u32[]{:S(2)}) %all-to-all-start.3) | async-done | bytes 2097184 | tf_op jit(solution)/shard_map/all_to_all | solution.py:168
  202.8 2.9 copy.71
  205.7 9.0 %fusion.38 = f32[512,8,128]{2,0,1:T(8,128)S(1)} fusion(f32[8,512,128]{2,1,0:T(8,128)} %bitcast.180), kind=kOutput, calls=%fused_computation.60 | convolution fusion | flops 3225157632 | bytes 4194304 | tf_op jit(solution)/shard_map/nyx,ym->nmx/dot_general | solution.py:170
  214.7 9.2 %bitcast_subtract_fusion.1 = (f32[8,512,128]{2,1,0:T(8,128)S(1)}, f32[512,8,128]{2,0,1:T(8,128)}) fusion(f32[512,8,128]{2,0,1:T(8,128)S(1)} %fusion.38, f32[8,512,128]{2,1,0:T(8,128)S(1)} %bitcast.175), kind=kOutput, calls=%fused_computation.22 | convolution fusion | flops 3225681920 | bytes 8388608 | tf_op jit(solution)/shard_map/nyx,ym->nmx/dot_general | solution.py:177
  223.9 2.6 copy.74
  226.4 5.2 %all-to-all-start.5 = ((f32[8,512,128]{2,0,1:T(8,128)}), f32[8,512,128]{2,0,1:T(8,128)S(1)}, u32[]{:S(2)}, u32[]{:S(2)}) async-start(f32[8,512,128]{2,0,1:T(8,128)} %copy.74), calls=%async_computation.5 | async-start | bytes 4194304 | tf_op jit(solution)/shard_map/all_to_all | solution.py:194
  231.7 11.1 %fusion.7 = f32[8,512,128]{2,1,0:T(8,128)S(1)} fusion(f32[512,8,128]{2,0,1:T(8,128)} %get-tuple-element.158, f32[512,8,128]{2,0,1:T(8,128)} %copy-done.4, f32[8,512,128]{2,1,0:T(8,128)} %bitcast.181, f32[8,512,128]{2,1,0:T(8,128)} %bitcast.176), kind=kOutput, calls=%fused_computation.21 | convolution fusion | flops 3227254784 | bytes 10485760 | tf_op jit(solution)/shard_map/nyx,ym->nmx/dot_general | solution.py:184
  242.8 2.5 copy.76
  245.3 34.3 %all-to-all-done.5 = f32[8,512,128]{2,0,1:T(8,128)S(1)} async-done(((f32[8,512,128]{2,0,1:T(8,128)}), f32[8,512,128]{2,0,1:T(8,128)S(1)}, u32[]{:S(2)}, u32[]{:S(2)}) %all-to-all-start.5) | async-done | bytes 2097184 | tf_op jit(solution)/shard_map/all_to_all | solution.py:194
  279.6 1.3 copy-done
  280.9 4.6 %all-to-all-start.6 = ((f32[8,512,128]{2,0,1:T(8,128)}), f32[8,512,128]{2,0,1:T(8,128)}, u32[]{:S(2)}, u32[]{:S(2)}) async-start(f32[8,512,128]{2,0,1:T(8,128)} %copy.76), calls=%async_computation.6 | async-start | bytes 4194304 | tf_op jit(solution)/shard_map/all_to_all | solution.py:195
  285.5 3.6 %fusion.5 = f32[64,64,128]{2,0,1:T(8,128)S(1)} fusion(f32[8,8,64,128]{3,0,2,1:T(8,128)} %bitcast.173), kind=kOutput, calls=%fused_computation.18 | convolution fusion | flops 402714624 | bytes 4194304 | tf_op jit(solution)/shard_map/zyx,zm->myx/dot_general | solution.py:196
  289.1 44.2 %all-to-all-done.6 = f32[8,512,128]{2,0,1:T(8,128)} async-done(((f32[8,512,128]{2,0,1:T(8,128)}), f32[8,512,128]{2,0,1:T(8,128)}, u32[]{:S(2)}, u32[]{:S(2)}) %all-to-all-start.6) | async-done | bytes 2097184 | tf_op jit(solution)/shard_map/all_to_all | solution.py:195
  333.3 3.7 %fusion.1 = f32[64,64,128]{2,0,1:T(8,128)S(1)} fusion(f32[8,8,64,128]{3,0,2,1:T(8,128)} %bitcast.93), kind=kOutput, calls=%fused_computation.14 | convolution fusion | flops 402714624 | bytes 4194304 | tf_op jit(solution)/shard_map/zyx,zm->myx/dot_general | solution.py:203
  337.1 3.9 %subtract_bitcast_fusion = f32[1,64,64,128]{3,1,2,0:T(8,128)S(1)} fusion(f32[64,64,128]{2,0,1:T(8,128)S(1)} %fusion.1, f32[64,64,128]{2,0,1:T(8,128)S(1)} %fusion.5, f32[8,8,64,128]{3,0,2,1:T(8,128)} %bitcast.93, f32[8,8,64,128]{3,0,2,1:T(8,128)S(1)} %bitcast.174), kind=kOutput, calls=%fused_computation.27 | convolution fusion | flops 404295680 | bytes 10485760 | tf_op jit(solution)/shard_map/zyx,zm->myx/dot_general | solution.py:210
  342.0 4.4 %copy.78 = f32[2,64,64,128]{3,2,1,0:T(8,128)} copy(f32[2,64,64,128]{3,1,2,0:T(8,128)S(1)} %pad_maximum_fusion) | data formatting | bytes 8388608 | tf_op jit(solution)/shard_map/stack | solution.py:219
  (78 shorter events, 6.1 us)
Async XLA Ops:
  0.0 42.0 %copy-start.6 = (f32[3,256]{1,0:T(4,128)S(1)}, f32[3,256]{1,0:T(4,128)}, u32[]{:S(2)}) copy-start(f32[3,256]{1,0:T(4,128)} %param.10) | copy-start | bytes 9220
  0.0 42.0 %copy-start.7 = (f32[2,256]{1,0:T(2,128)S(1)}, f32[2,256]{1,0:T(2,128)}, u32[]{:S(2)}) copy-start(f32[2,256]{1,0:T(2,128)} %param.11) | copy-start | bytes 6148
  34.7 13.8 %all-to-all-start = ((s32[8,1,384]{2,1,0:T(1,128)}), s32[8,1,384]{2,1,0:T(1,128)S(1)}, u32[]{:S(2)}, u32[]{:S(2)}) async-start(s32[8,1,384]{2,1,0:T(1,128)} %reshape.1138), calls=%async_computation | async-start | bytes 24576 | tf_op jit(solution)/shard_map/all_to_all | solution.py:141
  48.5 9.9 %all-to-all-start.1 = ((f32[8,1,640]{2,1,0:T(1,128)}), f32[8,1,640]{2,1,0:T(1,128)S(1)}, u32[]{:S(2)}, u32[]{:S(2)}) async-start(f32[8,1,640]{2,1,0:T(1,128)} %reshape.1134), calls=%async_computation.1 | async-start | bytes 40960 | tf_op jit(solution)/shard_map/all_to_all | solution.py:147
  53.3 3.9 %collective-permute-start.2 = (s32[3,8,1,32]{3,2,0,1:T(1,128)S(1)}, s32[3,8,1,32]{3,2,0,1:T(1,128)S(1)}, u32[]{:S(2)}, u32[]{:S(2)}) collective-permute-start(s32[3,8,1,32]{3,2,0,1:T(1,128)S(1)} %get-tuple-element.68), channel_id=1, source_target_pairs={{0,3},{1,2},{2,1},{3,0},{4,7},{5,6},{6,5},{7,4},{8,11},{9,10},{10,... | collective-permute-start | bytes 9224 | tf_op jit(solution)/shard_map/ppermute | solution.py:24
  53.5 3.7 %collective-permute-start.1 = (s32[3,8,1,32]{3,2,0,1:T(1,128)S(1)}, s32[3,8,1,32]{3,2,0,1:T(1,128)S(1)}, u32[]{:S(2)}, u32[]{:S(2)}) collective-permute-start(s32[3,8,1,32]{3,2,0,1:T(1,128)S(1)} %get-tuple-element.69), channel_id=1, source_target_pairs={{0,2},{1,3},{2,0},{3,1},{4,6},{5,7},{6,4},{7,5},{8,10},{9,11},{10,... | collective-permute-start | bytes 9224 | tf_op jit(solution)/shard_map/ppermute | solution.py:24
  55.0 1.2 collective-permute-start
  60.6 7.1 %all-to-all-start.2 = ((f32[4,1,1280]{2,1,0:T(1,128)}), f32[4,1,1280]{2,1,0:T(1,128)S(1)}, u32[]{:S(2)}, u32[]{:S(2)}) async-start(f32[4,1,1280]{2,1,0:T(1,128)} %reshape.1136), calls=%async_computation.2 | async-start | bytes 40960 | tf_op jit(solution)/shard_map/all_to_all | solution.py:146
  82.4 11.9 %copy-start.5 = (f32[8,135,1024]{2,1,0:T(8,128)S(1)}, f32[8,135,1024]{2,1,0:T(8,128)}, u32[]{:S(2)}) copy-start(f32[8,135,1024]{2,1,0:T(8,128)} %reshape.921) | copy-start | bytes 13271044
  104.0 5.8 %collective-permute-start.3 = (f32[2,8,7,512]{3,2,1,0:T(8,128)S(1)}, f32[2,8,7,512]{3,2,1,0:T(8,128)S(1)}, u32[]{:S(2)}, u32[]{:S(2)}) collective-permute-start(f32[2,8,7,512]{3,2,1,0:T(8,128)S(1)} %pad_maximum_fusion.1), channel_id=1, source_target_pairs={{3,0},{0,1},{1,2},{2,3},{7,4},{4,5},{5,6},{6,7},{11,8},{8,9},{9,10... | collective-permute-start | bytes 688136 | tf_op jit(solution)/shard_map/ppermute | solution.py:32
  141.9 29.2 %all-to-all-start.4 = ((f32[8,128,512]{1,0,2:T(8,128)}), f32[8,128,512]{1,0,2:T(8,128)S(1)}, u32[]{:S(2)}, u32[]{:S(2)}) async-start(f32[8,128,512]{1,0,2:T(8,128)} %copy.72), calls=%async_computation.4 | async-start | bytes 4194304 | tf_op jit(solution)/shard_map/all_to_all | solution.py:169
  171.1 1.3 copy-start.3
  172.5 30.3 %all-to-all-start.3 = ((f32[8,128,512]{1,0,2:T(8,128)}), f32[8,128,512]{1,0,2:T(8,128)}, u32[]{:S(2)}, u32[]{:S(2)}) async-start(f32[8,128,512]{1,0,2:T(8,128)} %copy.70), calls=%async_computation.3 | async-start | bytes 4194304 | tf_op jit(solution)/shard_map/all_to_all | solution.py:168
  179.0 35.6 %copy-start.2 = (f32[8,128,4,128]{3,1,2,0:T(8,128)}, f32[8,128,4,128]{3,1,2,0:T(8,128)S(1)}, u32[]{:S(2)}) copy-start(f32[8,128,4,128]{3,1,2,0:T(8,128)S(1)} %copy.73) | copy-start | bytes 6291460
  214.6 9.2 %copy-start.4 = (f32[512,8,128]{2,0,1:T(8,128)}, f32[512,8,128]{2,0,1:T(8,128)S(1)}, u32[]{:S(2)}) copy-start(f32[512,8,128]{2,0,1:T(8,128)S(1)} %fusion.38) | copy-start | bytes 6291460
  226.4 53.1 %all-to-all-start.5 = ((f32[8,512,128]{2,0,1:T(8,128)}), f32[8,512,128]{2,0,1:T(8,128)S(1)}, u32[]{:S(2)}, u32[]{:S(2)}) async-start(f32[8,512,128]{2,0,1:T(8,128)} %copy.74), calls=%async_computation.5 | async-start | bytes 4194304 | tf_op jit(solution)/shard_map/all_to_all | solution.py:194
  279.6 1.3 copy-start
  280.9 52.4 %all-to-all-start.6 = ((f32[8,512,128]{2,0,1:T(8,128)}), f32[8,512,128]{2,0,1:T(8,128)}, u32[]{:S(2)}, u32[]{:S(2)}) async-start(f32[8,512,128]{2,0,1:T(8,128)} %copy.76), calls=%async_computation.6 | async-start | bytes 4194304 | tf_op jit(solution)/shard_map/all_to_all | solution.py:195
  333.3 3.8 %copy-start.1 = (f32[8,512,128]{2,0,1:T(8,128)S(1)}, f32[8,512,128]{2,0,1:T(8,128)}, u32[]{:S(2)}) copy-start(f32[8,512,128]{2,0,1:T(8,128)} %copy-done) | copy-start | bytes 6291460
